TPU v7x, 32 devices: a whole 2x2x4 slice. The times are simulated.
32 devices in a mesh: traj: 16 (over z, y, core), tm: 2 (over x).
Axes of the slice: x: 2, y: 2, z: 4, core: 2. Of those that a mesh axis runs over, the one named last changes fastest.
Arguments:
- states: float32 [2, 32, 4096], P('tm', None, 'traj'), may hold values from -6 to 6
- vectors: bfloat16 [64, 4096], P(None, 'traj'), may hold values from -6 to 6
- kernel_scale: float32 [2], P('tm'), may hold values from 6 to 16
- neighbour_blocks: int32 [32, 24], P('traj'), may hold values from 0 to 31, as said below
- neighbour_count: int32 [32], P('traj'), may hold values from 6 to 24, as said below
Outputs:
- result: float32 [64, 4096], P(None, 'traj')
Inputs may be any that keep to these rules, and one draw needn't show every extreme that they name: `neighbour_blocks`: row b names 24 different blocks, the first of them b itself. Only the first neighbour_count[b] entries of row b of neighbour_blocks are neighbours of block b; some block uses all 24.
All inputs are finite; a program needn't handle non-finite values.
Results may differ from a plain program's by a relative error of at most 0.0013.
Values may be sent and summed in bfloat16 or wider, within the bound.
No kernel may reach another device: no remote copies, remote signals or barrier semaphores. Data moves between devices by JAX's collectives and lax.ppermute only.
A program may use at most 64 MiB of HBM per device.

v0:
```python
import math
import jax
import jax.numpy as jnp
from jax import lax
from jax.sharding import PartitionSpec as P

BLK = 128


def linked_blocks(neighbour_blocks, neighbour_count, blocks_total):
    slots = neighbour_blocks.shape[1]
    named = neighbour_blocks[:, :, None] == jnp.arange(blocks_total, dtype=jnp.int32)[None, None, :]
    within = jnp.arange(slots, dtype=jnp.int32)[None, :, None] < neighbour_count[:, None, None]
    return jnp.any(named & within, axis=1).astype(jnp.float32)


def per_device(states, vectors, kernel_scale, neighbour_blocks, neighbour_count):
    coords_all = lax.all_gather(states, "traj", axis=2, tiled=True)[0]
    vectors_all = lax.all_gather(vectors, "traj", axis=1, tiled=True)
    own = states[0]
    spread = kernel_scale[0]
    own_rows = own.shape[1]
    columns = coords_all.shape[1]
    vector_count = vectors.shape[0]
    blocks_total = columns // BLK
    block_rows = own_rows // BLK
    own_squares = jnp.sum(own * own, axis=0)
    all_squares = jnp.sum(coords_all * coords_all, axis=0)
    tile_width = math.gcd(columns, 512)
    tile_count = columns // tile_width
    linked = linked_blocks(neighbour_blocks, neighbour_count, blocks_total)

    def dense_kernel(tile_index):
        offset = tile_index * tile_width
        slab = lax.dynamic_slice_in_dim(coords_all, offset, tile_width, 1)
        cross = lax.dot_general(
            own, slab, (((0,), (0,)), ((), ())), precision=lax.Precision.HIGHEST
        )
        slab_squares = lax.dynamic_slice_in_dim(all_squares, offset, tile_width, 0)
        distance = own_squares[:, None] + slab_squares[None, :] - 2.0 * cross
        mask = lax.dynamic_slice_in_dim(linked, offset // BLK, tile_width // BLK, 1)
        shaped = jnp.exp(-distance / spread).reshape(block_rows, BLK, tile_width // BLK, BLK)
        return (mask[:, None, :, None] * shaped).reshape(own_rows, tile_width)

    def first_dense(tile_index, carry):
        row_sum, pushed = carry
        kernel = dense_kernel(tile_index)
        weights = kernel.astype(jnp.bfloat16)
        slab_vectors = lax.dynamic_slice_in_dim(vectors_all, tile_index * tile_width, tile_width, 1)
        pushed = pushed + lax.dot_general(
            slab_vectors, weights, (((1,), (1,)), ((), ())), preferred_element_type=jnp.float32
        )
        return (row_sum + jnp.sum(kernel, axis=1), pushed)

    row_sum, pushed = lax.fori_loop(
        0,
        tile_count,
        first_dense,
        (jnp.zeros((own_rows,), jnp.float32), jnp.zeros((vector_count, own_rows), jnp.float32)),
    )
    scaled = (pushed / (row_sum * row_sum)[None, :]).astype(jnp.bfloat16)
    lists_whole, counts_whole = (
        lax.all_gather(neighbour_blocks, "traj", axis=0, tiled=True),
        lax.all_gather(neighbour_count, "traj", axis=0, tiled=True),
    )
    linked_whole = linked_blocks(lists_whole, counts_whole, blocks_total)
    own_start = lax.axis_index("traj") * block_rows
    column_mask = lax.dynamic_slice_in_dim(linked_whole, own_start, block_rows, 1)
    scaled_whole = lax.all_gather(scaled, "traj", axis=1, tiled=True)

    def pull_tile(tile_index, total):
        offset = tile_index * tile_width
        slab = lax.dynamic_slice_in_dim(coords_all, offset, tile_width, 1)
        cross = lax.dot_general(
            slab, own, (((0,), (0,)), ((), ())), precision=lax.Precision.HIGHEST
        )
        slab_squares = lax.dynamic_slice_in_dim(all_squares, offset, tile_width, 0)
        distance = slab_squares[:, None] + own_squares[None, :] - 2.0 * cross
        mask = lax.dynamic_slice_in_dim(column_mask, offset // BLK, tile_width // BLK, 0)
        shaped = jnp.exp(-distance / spread).reshape(tile_width // BLK, BLK, block_rows, BLK)
        weights = (
            (mask[:, None, :, None] * shaped).reshape(tile_width, own_rows).astype(jnp.bfloat16)
        )
        slab_scaled = lax.dynamic_slice_in_dim(scaled_whole, offset, tile_width, 1)
        return total + jnp.dot(slab_scaled, weights, preferred_element_type=jnp.float32)

    own_pulled = lax.fori_loop(
        0, tile_count, pull_tile, jnp.zeros((vector_count, own_rows), jnp.float32)
    )
    result = lax.psum(own_pulled, "tm")
    return result


def solution(mesh):
    in_specs = (P("tm", None, "traj"), P(None, "traj"), P("tm"), P("traj", None), P("traj"))
    out_specs = P(None, "traj")
    return jax.shard_map(
        per_device, mesh=mesh, in_specs=in_specs, out_specs=out_specs, check_vma=False
    )
```

profile of v0, /device:TPU:0, one launch (start us, length us, event | category | flops | bytes accessed | tf_op | source)
XLA Modules:
  0.0 164.4 jit_solution(14845167993915511679)
XLA Ops:
  6.5 24.9 %all_gather.15 = f32[1,32,4096]{2,1,0:T(8,128)S(1)} all-gather(f32[1,32,256]{2,1,0:T(8,128)} %param.9), channel_id=1, replica_groups=mesh['traj'=16,'tm'=2] {'traj'}, dimensions={2}, use_global_device_ids=true | all-gather | bytes 557056 | tf_op jit(solution)/shard_map/all_gather | solution.py:18
  32.3 19.0 %all_gather.16 = bf16[64,4096]{1,0:T(8,128)(2,1)S(1)} all-gather(bf16[64,256]{1,0:T(8,128)(2,1)S(1)} %copy-done.2), channel_id=1, replica_groups=mesh['traj'=16,'tm'=2] {'traj'}, dimensions={1}, use_global_device_ids=true | all-gather | bytes 557056 | tf_op jit(solution)/shard_map/all_gather | solution.py:19
  52.1 17.0 %while.34 = (s32[]{:T(128)}, f32[256]{0:T(256)S(1)}, f32[64,256]{1,0:T(8,128)S(1)}, f32[2,32]{1,0:T(2,128)S(1)}, f32[256]{0:T(256)S(1)}, /*index=5*/f32[4096]{0:...) while((s32[]{:T(128)}, f32[256]{0:T(256)S(1)}, ...), condition=%wide.region_6.7_spmd.clone, body=%wide.region_4.0_spmd.clone.sunk | while | flops 68190488 | bytes 1879617 | solution.py:55
  52.6 1.4 fusion.42
  54.7 1.4 fusion.42
  56.8 1.4 fusion.42
  59.0 1.4 fusion.42
  61.1 1.4 fusion.42
  63.2 1.4 fusion.42
  65.4 1.4 fusion.42
  67.5 1.4 fusion.42
  69.1 20.3 %all_gather.17 = bf16[64,4096]{1,0:T(8,128)(2,1)S(1)} all-gather(bf16[64,256]{1,0:T(8,128)(2,1)S(1)} %divide_convert_fusion), channel_id=1, replica_groups=mesh['traj'=16,'tm'=2] {'traj'}, dimensions={1}, use_global_device_ids=true | all-gather | bytes 557056 | tf_op jit(solution)/shard_map/all_gather | solution.py:69
  91.7 8.0 %all-reduce = s32[32]{0:T(128)S(1)} all-reduce(s32[32]{0:T(128)S(1)} %dynamic-update-slice), channel_id=1, replica_groups=mesh['traj'=16,'tm'=2] {'traj'}, use_global_device_ids=true, to_apply=%add | all-reduce | flops 32 | bytes 256
  99.8 21.6 %all-gather = s32[16,2,24]{2,1,0:T(2,128)S(1)} all-gather(s32[1,2,24]{2,1,0:T(2,128)S(1)} %bitcast.53), channel_id=1, replica_groups=mesh['traj'=16,'tm'=2] {'traj'}, dimensions={0}, use_global_device_ids=true | all-gather | bytes 3264 | tf_op jit(solution)/shard_map/all_gather | solution.py:63
  121.7 15.4 %while.35 = (s32[]{:T(128)}, f32[64,256]{1,0:T(8,128)S(1)}, bf16[64,4096]{1,0:T(8,128)(2,1)S(1)}, f32[32,2]{1,0:T(8,128)S(1)}, f32[4096]{0:T(1024)S(1)}, /*index...) while((s32[]{:T(128)}, f32[64,256]{1,0:T(8,128)S(1)}, ...), condition=%wide.region_8.9_spmd.clone, body=%wide.region_7.8_spmd.clone.sunk | while | flops 68059160 | bytes 1875448 | solution.py:87
  122.0 1.4 fusion.47
  124.0 1.4 fusion.47
  125.9 1.4 fusion.47
  129.8 1.4 fusion.47
  131.7 1.4 fusion.47
  133.6 1.4 fusion.47
  135.5 1.4 fusion.47
  137.8 18.3 %all-reduce.3.cloned.1.call-done = f32[64,256]{1,0:T(8,128)} async-done(((f32[64,256]{1,0:T(8,128)}), f32[64,256]{1,0:T(8,128)}) %all-reduce.3.cloned.1.call-update) | async-done | bytes 65552 | tf_op jit(solution)/shard_map/psum | solution.py:90
  156.1 1.5 copy.35
  (111 shorter events, 14.7 us)
Async XLA Ops:
  6.5 24.9 %copy-start.1 = (f32[1,32,256]{2,1,0:T(8,128)S(1)}, f32[1,32,256]{2,1,0:T(8,128)}, u32[]{:S(2)}) copy-start(f32[1,32,256]{2,1,0:T(8,128)} %param.9) | copy-start | bytes 98308
  6.5 149.6 %all-reduce.3.cloned.1.call-start = ((), (), s32[]{:S(2)}) async-start(), calls=%async_computation | async-start | bytes 131072 | tf_op jit(solution)/shard_map/psum | solution.py:90
  31.5 0.8 copy-start.2
  32.3 19.0 %copy-start.4 = (s32[2]{0:T(128)S(1)}, s32[2]{0:T(128)}, u32[]{:S(2)}) copy-start(s32[2]{0:T(128)} %param.13) | copy-start | bytes 28
  51.3 0.7 copy-start.3
  89.5 0.7 copy-start.5
  137.1 0.6 copy-start
Sparse Core Ops, SparseCore 0:
  137.9 18.1 all-reduce.2
where the time goes:
time: 165 us; the launch traced here: 164 us
  blocking collectives  93.8 us (57%)
  matrix products  25.1 us (15%)
  waiting for transfers between devices  18.4 us (11%)
  between operations  14.2 us (9%)
  local copies, waits for them, and re-layouts  10.9 us (7%)
    all_gather x1, blocking collectives, per_device(): coords_all = lax.all_gather(states, 'traj', axis=2, tiled=True)[0]  24.9 us
    all_gather x1, blocking collectives, per_device(): lax.all_gather(neighbour_blocks, 'traj', axis=0, tiled=True)  21.6 us
    all_gather x1, blocking collectives, per_device(): scaled_whole = lax.all_gather(scaled, 'traj', axis=1, tiled=True)  20.3 us
    all_gather x1, blocking collectives, per_device(): vectors_all = lax.all_gather(vectors, 'traj', axis=1, tiled=True)  19 us
    psum x1, waiting for transfers between devices, per_device(): result = lax.psum(own_pulled, 'tm')  18.3 us
    dot_general x8, matrix products, dense_kernel(): lax.dot_general(own, slab, (((0,), (0,)), ((), ())), precision=lax.Precis...  11.2 us
    dot_general x8, matrix products, pull_tile(): lax.dot_general(slab, own, (((0,), (0,)), ((), ())), precision=lax.Precis...  10.9 us
    unnamed x1, blocking collectives  7.97 us
  transfers between devices with their start and end apart: 1, of which 1 were waited for; matrix products, arithmetic and copies ran while one was open for 0% of the time, Pallas kernels for 0%

commit v1 on v0

--- a/solution.py
+++ b/solution.py
@@ -66,7 +66,24 @@
     linked_whole = linked_blocks(lists_whole, counts_whole, blocks_total)
     own_start = lax.axis_index("traj") * block_rows
     column_mask = lax.dynamic_slice_in_dim(linked_whole, own_start, block_rows, 1)
-    scaled_whole = lax.all_gather(scaled, "traj", axis=1, tiled=True)
+
+    def mix_the_trees(matrix, named_axis):
+        parts_n = jax.lax.axis_size(named_axis)
+        in_order = []
+        t = 0
+        while t < parts_n:
+            in_order.append((t, (t + 1) % parts_n))
+            t += 1
+        state_next = [None] * parts_n
+        state_next[parts_n - 1] = matrix
+        for p in range(parts_n - 2, -1, -1):
+            state_next[p] = jax.lax.ppermute(state_next[p + 1], named_axis, in_order)
+        mid_arr = jnp.concatenate(state_next, 1)
+        oldest = jax.lax.axis_index(named_axis)
+        left_arr = (oldest + 1) * matrix.shape[1]
+        return jnp.roll(mid_arr, left_arr, 1)
+
+    scaled_whole = mix_the_trees(scaled, "traj")
 
     def pull_tile(tile_index, total):
         offset = tile_index * tile_width

time: 165 us -> 224 us (1.36)
  waiting for transfers between devices: 18.4 us -> 95.9 us
  blocking collectives: 93.8 us -> 74 us
    ppermute x0 -> x15, waiting for transfers between devices: none -> 77.6 us  [mix_the_trees(): state_next[p] = jax.lax.ppermute(state_next[p + 1], named_axis, in_order)]
    all_gather x1 -> x0, blocking collectives: 20.3 us -> none  [per_device(): scaled_whole = lax.all_gather(scaled, 'traj', axis=1, tiled=True)]
    unnamed x1, blocking collectives: 7.97 us -> 12.1 us
    all_gather x1, blocking collectives: 21.6 us -> 18 us  [per_device(): lax.all_gather(neighbour_blocks, 'traj', axis=0, tiled=True)]
    unnamed x16 -> x46, local copies, waits for them, and re-layouts: 4.95 us -> 5.01 us
  transfers between devices with their start and end apart: 1 -> 16, of which waited for: 1 -> 14; matrix products, arithmetic and copies ran while one was open for 0% -> 1% of each run, Pallas kernels for 0% -> 0%
where the time goes in v1:
time: 224 us; the launch traced here: 223 us
  waiting for transfers between devices  95.9 us (43%)
  blocking collectives  74 us (33%)
  matrix products  25.1 us (11%)
  between operations  14.4 us (6%)
  local copies, waits for them, and re-layouts  11 us (5%)
    ppermute x15, waiting for transfers between devices, mix_the_trees(): state_next[p] = jax.lax.ppermute(state_next[p + 1], named_axis, in_order)  77.6 us
    all_gather x1, blocking collectives, per_device(): coords_all = lax.all_gather(states, 'traj', axis=2, tiled=True)[0]  24.9 us
    all_gather x1, blocking collectives, per_device(): vectors_all = lax.all_gather(vectors, 'traj', axis=1, tiled=True)  19 us
    psum x1, waiting for transfers between devices, per_device(): result = lax.psum(own_pulled, 'tm')  18.4 us
    all_gather x1, blocking collectives, per_device(): lax.all_gather(neighbour_blocks, 'traj', axis=0, tiled=True)  18 us
    unnamed x1, blocking collectives  12.1 us
    dot_general x8, matrix products, dense_kernel(): lax.dot_general(own, slab, (((0,), (0,)), ((), ())), precision=lax.Precis...  11.2 us
    dot_general x8, matrix products, pull_tile(): lax.dot_general(slab, own, (((0,), (0,)), ((), ())), precision=lax.Precis...  10.9 us
  transfers between devices with their start and end apart: 16, of which 14 were waited for; matrix products, arithmetic and copies ran while one was open for 1% of the time, Pallas kernels for 0%

profile of v1, /device:TPU:0, one launch (start us, length us, event | category | flops | bytes accessed | tf_op | source)
XLA Modules:
  0.0 223.2 jit_solution(12753077875305303366)
XLA Ops:
  6.5 24.9 %all_gather.12 = f32[1,32,4096]{2,1,0:T(8,128)S(1)} all-gather(f32[1,32,256]{2,1,0:T(8,128)} %param.9), channel_id=1, replica_groups=mesh['traj'=16,'tm'=2] {'traj'}, dimensions={2}, use_global_device_ids=true | all-gather | bytes 557056 | tf_op jit(solution)/shard_map/all_gather | solution.py:18
  32.3 19.0 %all_gather.13 = bf16[64,4096]{1,0:T(8,128)(2,1)S(1)} all-gather(bf16[64,256]{1,0:T(8,128)(2,1)S(1)} %copy-done.2), channel_id=1, replica_groups=mesh['traj'=16,'tm'=2] {'traj'}, dimensions={1}, use_global_device_ids=true | all-gather | bytes 557056 | tf_op jit(solution)/shard_map/all_gather | solution.py:19
  52.1 17.0 %while.34 = (s32[]{:T(128)}, f32[256]{0:T(256)S(1)}, f32[64,256]{1,0:T(8,128)S(1)}, f32[2,32]{1,0:T(2,128)S(1)}, f32[256]{0:T(256)S(1)}, /*index=5*/f32[4096]{0:...) while((s32[]{:T(128)}, f32[256]{0:T(256)S(1)}, ...), condition=%wide.region_6.7_spmd.clone, body=%wide.region_4.0_spmd.clone.sunk | while | flops 68190488 | bytes 1879617 | solution.py:55
  52.6 1.4 fusion.42
  54.7 1.4 fusion.42
  63.2 1.4 fusion.42
  69.5 5.7 %collective-permute-done = bf16[64,256]{1,0:T(8,128)(2,1)S(1)} collective-permute-done((bf16[64,256]{1,0:T(8,128)(2,1)S(1)}, bf16[64,256]{1,0:T(8,128)(2,1)S(1)}, u32[]{:S(2)}, u32[]{:S(2)}) %collective-permute-start) | collective-permute-done | bytes 32800 | tf_op jit(solution)/shard_map/ppermute | solution.py:80
  75.2 6.0 %collective-permute-done.1 = bf16[64,256]{1,0:T(8,128)(2,1)S(1)} collective-permute-done((bf16[64,256]{1,0:T(8,128)(2,1)S(1)}, bf16[64,256]{1,0:T(8,128)(2,1)S(1)}, u32[]{:S(2)}, u32[]{:S(2)}) %collective-permute-start.1) | collective-permute-done | bytes 32800 | tf_op jit(solution)/shard_map/ppermute | solution.py:80
  81.3 6.0 %collective-permute-done.2 = bf16[64,256]{1,0:T(8,128)(2,1)S(1)} collective-permute-done((bf16[64,256]{1,0:T(8,128)(2,1)S(1)}, bf16[64,256]{1,0:T(8,128)(2,1)S(1)}, u32[]{:S(2)}, u32[]{:S(2)}) %collective-permute-start.2) | collective-permute-done | bytes 32800 | tf_op jit(solution)/shard_map/ppermute | solution.py:80
  87.3 6.0 %collective-permute-done.3 = bf16[64,256]{1,0:T(8,128)(2,1)S(1)} collective-permute-done((bf16[64,256]{1,0:T(8,128)(2,1)S(1)}, bf16[64,256]{1,0:T(8,128)(2,1)S(1)}, u32[]{:S(2)}, u32[]{:S(2)}) %collective-permute-start.3) | collective-permute-done | bytes 32800 | tf_op jit(solution)/shard_map/ppermute | solution.py:80
  93.3 6.0 %collective-permute-done.4 = bf16[64,256]{1,0:T(8,128)(2,1)S(1)} collective-permute-done((bf16[64,256]{1,0:T(8,128)(2,1)S(1)}, bf16[64,256]{1,0:T(8,128)(2,1)S(1)}, u32[]{:S(2)}, u32[]{:S(2)}) %collective-permute-start.4) | collective-permute-done | bytes 32800 | tf_op jit(solution)/shard_map/ppermute | solution.py:80
  99.4 6.0 %collective-permute-done.5 = bf16[64,256]{1,0:T(8,128)(2,1)S(1)} collective-permute-done((bf16[64,256]{1,0:T(8,128)(2,1)S(1)}, bf16[64,256]{1,0:T(8,128)(2,1)S(1)}, u32[]{:S(2)}, u32[]{:S(2)}) %collective-permute-start.5) | collective-permute-done | bytes 32800 | tf_op jit(solution)/shard_map/ppermute | solution.py:80
  105.4 6.0 %collective-permute-done.6 = bf16[64,256]{1,0:T(8,128)(2,1)S(1)} collective-permute-done((bf16[64,256]{1,0:T(8,128)(2,1)S(1)}, bf16[64,256]{1,0:T(8,128)(2,1)S(1)}, u32[]{:S(2)}, u32[]{:S(2)}) %collective-permute-start.6) | collective-permute-done | bytes 32800 | tf_op jit(solution)/shard_map/ppermute | solution.py:80
  111.4 6.0 %collective-permute-done.7 = bf16[64,256]{1,0:T(8,128)(2,1)S(1)} collective-permute-done((bf16[64,256]{1,0:T(8,128)(2,1)S(1)}, bf16[64,256]{1,0:T(8,128)(2,1)S(1)}, u32[]{:S(2)}, u32[]{:S(2)}) %collective-permute-start.7) | collective-permute-done | bytes 32800 | tf_op jit(solution)/shard_map/ppermute | solution.py:80
  117.5 6.0 %collective-permute-done.8 = bf16[64,256]{1,0:T(8,128)(2,1)S(1)} collective-permute-done((bf16[64,256]{1,0:T(8,128)(2,1)S(1)}, bf16[64,256]{1,0:T(8,128)(2,1)S(1)}, u32[]{:S(2)}, u32[]{:S(2)}) %collective-permute-start.8) | collective-permute-done | bytes 32800 | tf_op jit(solution)/shard_map/ppermute | solution.py:80
  123.5 6.0 %collective-permute-done.9 = bf16[64,256]{1,0:T(8,128)(2,1)S(1)} collective-permute-done((bf16[64,256]{1,0:T(8,128)(2,1)S(1)}, bf16[64,256]{1,0:T(8,128)(2,1)S(1)}, u32[]{:S(2)}, u32[]{:S(2)}) %collective-permute-start.9) | collective-permute-done | bytes 32800 | tf_op jit(solution)/shard_map/ppermute | solution.py:80
  129.6 6.0 %collective-permute-done.10 = bf16[64,256]{1,0:T(8,128)(2,1)S(1)} collective-permute-done((bf16[64,256]{1,0:T(8,128)(2,1)S(1)}, bf16[64,256]{1,0:T(8,128)(2,1)S(1)}, u32[]{:S(2)}, u32[]{:S(2)}) %collective-permute-start.10) | collective-permute-done | bytes 32800 | tf_op jit(solution)/shard_map/ppermute | solution.py:80
  137.7 12.1 %all-reduce = s32[32]{0:T(128)S(1)} all-reduce(s32[32]{0:T(128)S(1)} %dynamic-update-slice), channel_id=1, replica_groups=mesh['traj'=16,'tm'=2] {'traj'}, use_global_device_ids=true, to_apply=%add | all-reduce | flops 32 | bytes 256
  149.9 18.0 %all-gather = s32[16,2,24]{2,1,0:T(2,128)S(1)} all-gather(s32[1,2,24]{2,1,0:T(2,128)S(1)} %bitcast.53), channel_id=1, replica_groups=mesh['traj'=16,'tm'=2] {'traj'}, dimensions={0}, use_global_device_ids=true | all-gather | bytes 3264 | tf_op jit(solution)/shard_map/all_gather | solution.py:63
  168.4 5.6 %collective-permute-done.13 = bf16[64,256]{1,0:T(8,128)(2,1)S(1)} collective-permute-done((bf16[64,256]{1,0:T(8,128)(2,1)S(1)}, bf16[64,256]{1,0:T(8,128)(2,1)S(1)}, u32[]{:S(2)}, u32[]{:S(2)}) %collective-permute-start.13) | collective-permute-done | bytes 32800 | tf_op jit(solution)/shard_map/ppermute | solution.py:80
  174.0 6.0 %collective-permute-done.14 = bf16[64,256]{1,0:T(8,128)(2,1)S(1)} collective-permute-done((bf16[64,256]{1,0:T(8,128)(2,1)S(1)}, bf16[64,256]{1,0:T(8,128)(2,1)S(1)}, u32[]{:S(2)}, u32[]{:S(2)}) %collective-permute-start.14) | collective-permute-done | bytes 32800 | tf_op jit(solution)/shard_map/ppermute | solution.py:80
  180.4 15.4 %while.35 = (s32[]{:T(128)}, f32[64,256]{1,0:T(8,128)S(1)}, bf16[64,4096]{1,0:T(8,128)(2,1)S(1)}, f32[32,2]{1,0:T(8,128)S(1)}, f32[4096]{0:T(1024)S(1)}, /*index...) while((s32[]{:T(128)}, f32[64,256]{1,0:T(8,128)S(1)}, ...), condition=%wide.region_8.9_spmd.clone, body=%wide.region_7.8_spmd.clone.sunk | while | flops 68059160 | bytes 1875448 | solution.py:104
  196.5 18.4 %all-reduce.3.cloned.1.call-done = f32[64,256]{1,0:T(8,128)} async-done(((f32[64,256]{1,0:T(8,128)}), f32[64,256]{1,0:T(8,128)}) %all-reduce.3.cloned.1.call-update) | async-done | bytes 65552 | tf_op jit(solution)/shard_map/psum | solution.py:107
  214.9 1.5 copy.66
  (173 shorter events, 31.9 us)
Async XLA Ops:
  6.5 24.9 %copy-start.1 = (f32[1,32,256]{2,1,0:T(8,128)S(1)}, f32[1,32,256]{2,1,0:T(8,128)}, u32[]{:S(2)}) copy-start(f32[1,32,256]{2,1,0:T(8,128)} %param.9) | copy-start | bytes 98308
  6.5 208.4 %all-reduce.3.cloned.1.call-start = ((), (), s32[]{:S(2)}) async-start(), calls=%async_computation | async-start | bytes 131072 | tf_op jit(solution)/shard_map/psum | solution.py:107
  31.5 0.8 copy-start.2
  32.3 19.0 %copy-start.4 = (s32[2]{0:T(128)S(1)}, s32[2]{0:T(128)}, u32[]{:S(2)}) copy-start(s32[2]{0:T(128)} %param.13) | copy-start | bytes 28
  51.3 0.7 copy-start.3
  69.1 6.1 %collective-permute-start = (bf16[64,256]{1,0:T(8,128)(2,1)S(1)}, bf16[64,256]{1,0:T(8,128)(2,1)S(1)}, u32[]{:S(2)}, u32[]{:S(2)}) collective-permute-start(bf16[64,256]{1,0:T(8,128)(2,1)S(1)} %divide_convert_fusion), channel_id=1, source_target_pairs={{0,2},{2,4},{4,6},{6,8},{8,10},{10,12},{12,14},{14,16},{16,18},{18... | collective-permute-start | bytes 98312 | tf_op jit(solution)/shard_map/ppermute | solution.py:80
  75.2 6.0 %collective-permute-start.1 = (bf16[64,256]{1,0:T(8,128)(2,1)S(1)}, bf16[64,256]{1,0:T(8,128)(2,1)S(1)}, u32[]{:S(2)}, u32[]{:S(2)}) collective-permute-start(bf16[64,256]{1,0:T(8,128)(2,1)S(1)} %collective-permute-done), channel_id=1, source_target_pairs={{0,2},{2,4},{4,6},{6,8},{8,10},{10,12},{12,14},{14,16},{16,18},{18... | collective-permute-start | bytes 98312 | tf_op jit(solution)/shard_map/ppermute | solution.py:80
  81.2 6.0 %collective-permute-start.2 = (bf16[64,256]{1,0:T(8,128)(2,1)S(1)}, bf16[64,256]{1,0:T(8,128)(2,1)S(1)}, u32[]{:S(2)}, u32[]{:S(2)}) collective-permute-start(bf16[64,256]{1,0:T(8,128)(2,1)S(1)} %collective-permute-done.1), channel_id=1, source_target_pairs={{0,2},{2,4},{4,6},{6,8},{8,10},{10,12},{12,14},{14,16},{16,18},{18... | collective-permute-start | bytes 98312 | tf_op jit(solution)/shard_map/ppermute | solution.py:80
  87.3 6.0 %collective-permute-start.3 = (bf16[64,256]{1,0:T(8,128)(2,1)S(1)}, bf16[64,256]{1,0:T(8,128)(2,1)S(1)}, u32[]{:S(2)}, u32[]{:S(2)}) collective-permute-start(bf16[64,256]{1,0:T(8,128)(2,1)S(1)} %collective-permute-done.2), channel_id=1, source_target_pairs={{0,2},{2,4},{4,6},{6,8},{8,10},{10,12},{12,14},{14,16},{16,18},{18... | collective-permute-start | bytes 98312 | tf_op jit(solution)/shard_map/ppermute | solution.py:80
  93.3 6.0 %collective-permute-start.4 = (bf16[64,256]{1,0:T(8,128)(2,1)S(1)}, bf16[64,256]{1,0:T(8,128)(2,1)S(1)}, u32[]{:S(2)}, u32[]{:S(2)}) collective-permute-start(bf16[64,256]{1,0:T(8,128)(2,1)S(1)} %collective-permute-done.3), channel_id=1, source_target_pairs={{0,2},{2,4},{4,6},{6,8},{8,10},{10,12},{12,14},{14,16},{16,18},{18... | collective-permute-start | bytes 98312 | tf_op jit(solution)/shard_map/ppermute | solution.py:80
  99.4 6.0 %collective-permute-start.5 = (bf16[64,256]{1,0:T(8,128)(2,1)S(1)}, bf16[64,256]{1,0:T(8,128)(2,1)S(1)}, u32[]{:S(2)}, u32[]{:S(2)}) collective-permute-start(bf16[64,256]{1,0:T(8,128)(2,1)S(1)} %collective-permute-done.4), channel_id=1, source_target_pairs={{0,2},{2,4},{4,6},{6,8},{8,10},{10,12},{12,14},{14,16},{16,18},{18... | collective-permute-start | bytes 98312 | tf_op jit(solution)/shard_map/ppermute | solution.py:80
  105.4 6.0 %collective-permute-start.6 = (bf16[64,256]{1,0:T(8,128)(2,1)S(1)}, bf16[64,256]{1,0:T(8,128)(2,1)S(1)}, u32[]{:S(2)}, u32[]{:S(2)}) collective-permute-start(bf16[64,256]{1,0:T(8,128)(2,1)S(1)} %collective-permute-done.5), channel_id=1, source_target_pairs={{0,2},{2,4},{4,6},{6,8},{8,10},{10,12},{12,14},{14,16},{16,18},{18... | collective-permute-start | bytes 98312 | tf_op jit(solution)/shard_map/ppermute | solution.py:80
  111.4 6.0 %collective-permute-start.7 = (bf16[64,256]{1,0:T(8,128)(2,1)S(1)}, bf16[64,256]{1,0:T(8,128)(2,1)S(1)}, u32[]{:S(2)}, u32[]{:S(2)}) collective-permute-start(bf16[64,256]{1,0:T(8,128)(2,1)S(1)} %collective-permute-done.6), channel_id=1, source_target_pairs={{0,2},{2,4},{4,6},{6,8},{8,10},{10,12},{12,14},{14,16},{16,18},{18... | collective-permute-start | bytes 98312 | tf_op jit(solution)/shard_map/ppermute | solution.py:80
  117.5 6.0 %collective-permute-start.8 = (bf16[64,256]{1,0:T(8,128)(2,1)S(1)}, bf16[64,256]{1,0:T(8,128)(2,1)S(1)}, u32[]{:S(2)}, u32[]{:S(2)}) collective-permute-start(bf16[64,256]{1,0:T(8,128)(2,1)S(1)} %collective-permute-done.7), channel_id=1, source_target_pairs={{0,2},{2,4},{4,6},{6,8},{8,10},{10,12},{12,14},{14,16},{16,18},{18... | collective-permute-start | bytes 98312 | tf_op jit(solution)/shard_map/ppermute | solution.py:80
  123.5 6.0 %collective-permute-start.9 = (bf16[64,256]{1,0:T(8,128)(2,1)S(1)}, bf16[64,256]{1,0:T(8,128)(2,1)S(1)}, u32[]{:S(2)}, u32[]{:S(2)}) collective-permute-start(bf16[64,256]{1,0:T(8,128)(2,1)S(1)} %collective-permute-done.8), channel_id=1, source_target_pairs={{0,2},{2,4},{4,6},{6,8},{8,10},{10,12},{12,14},{14,16},{16,18},{18... | collective-permute-start | bytes 98312 | tf_op jit(solution)/shard_map/ppermute | solution.py:80
  129.5 6.0 %collective-permute-start.10 = (bf16[64,256]{1,0:T(8,128)(2,1)S(1)}, bf16[64,256]{1,0:T(8,128)(2,1)S(1)}, u32[]{:S(2)}, u32[]{:S(2)}) collective-permute-start(bf16[64,256]{1,0:T(8,128)(2,1)S(1)} %collective-permute-done.9), channel_id=1, source_target_pairs={{0,2},{2,4},{4,6},{6,8},{8,10},{10,12},{12,14},{14,16},{16,18},{18... | collective-permute-start | bytes 98312 | tf_op jit(solution)/shard_map/ppermute | solution.py:80
  135.6 14.2 %collective-permute-start.11 = (bf16[64,256]{1,0:T(8,128)(2,1)S(1)}, bf16[64,256]{1,0:T(8,128)(2,1)S(1)}, u32[]{:S(2)}, u32[]{:S(2)}) collective-permute-start(bf16[64,256]{1,0:T(8,128)(2,1)S(1)} %collective-permute-done.10), channel_id=1, source_target_pairs={{0,2},{2,4},{4,6},{6,8},{8,10},{10,12},{12,14},{14,16},{16,18},{18... | collective-permute-start | bytes 98312 | tf_op jit(solution)/shard_map/ppermute | solution.py:80
  135.6 0.7 copy-start.5
  149.8 18.1 %collective-permute-start.12 = (bf16[64,256]{1,0:T(8,128)(2,1)S(1)}, bf16[64,256]{1,0:T(8,128)(2,1)S(1)}, u32[]{:S(2)}, u32[]{:S(2)}) collective-permute-start(bf16[64,256]{1,0:T(8,128)(2,1)S(1)} %collective-permute-done.11), channel_id=1, source_target_pairs={{0,2},{2,4},{4,6},{6,8},{8,10},{10,12},{12,14},{14,16},{16,18},{18... | collective-permute-start | bytes 98312 | tf_op jit(solution)/shard_map/ppermute | solution.py:80
  167.9 6.0 %collective-permute-start.13 = (bf16[64,256]{1,0:T(8,128)(2,1)S(1)}, bf16[64,256]{1,0:T(8,128)(2,1)S(1)}, u32[]{:S(2)}, u32[]{:S(2)}) collective-permute-start(bf16[64,256]{1,0:T(8,128)(2,1)S(1)} %collective-permute-done.12), channel_id=1, source_target_pairs={{0,2},{2,4},{4,6},{6,8},{8,10},{10,12},{12,14},{14,16},{16,18},{18... | collective-permute-start | bytes 98312 | tf_op jit(solution)/shard_map/ppermute | solution.py:80
  173.9 6.0 %collective-permute-start.14 = (bf16[64,256]{1,0:T(8,128)(2,1)S(1)}, bf16[64,256]{1,0:T(8,128)(2,1)S(1)}, u32[]{:S(2)}, u32[]{:S(2)}) collective-permute-start(bf16[64,256]{1,0:T(8,128)(2,1)S(1)} %collective-permute-done.13), channel_id=1, source_target_pairs={{0,2},{2,4},{4,6},{6,8},{8,10},{10,12},{12,14},{14,16},{16,18},{18... | collective-permute-start | bytes 98312 | tf_op jit(solution)/shard_map/ppermute | solution.py:80
  195.9 0.6 copy-start
Sparse Core Ops, SparseCore 0:
  196.6 18.2 all-reduce.2
